TPU v7x, 512 devices: a 4x2x32 block of a 4x8x32 slice. The times are simulated.
512 devices in a mesh: parts: 2 (over y), seq: 32 (over z), head: 8 (over x, core).
Axes of the slice: x: 4, y: 2, z: 32, core: 2. Of those that a mesh axis runs over, the one named last changes fastest.
The devices are a block of a 4x8x32 slice.
Arguments:
- hidden: bfloat16 [48, 12288], P(('parts', 'head'), 'seq'), parts along dimension 0, may hold values from -600 to 600
- norm_gain: float32 [12288], P('seq'), may hold values from 0.1 to 1.9
- w_query: bfloat16 [12288, 12288], P('seq', 'head'), may hold values from -0.0546875 to 0.0546875
- w_key: bfloat16 [12288, 1024], P('seq', 'head'), may hold values from -0.0546875 to 0.0546875
- w_value: bfloat16 [12288, 1024], P('seq', 'head'), may hold values from -0.0546875 to 0.0546875
- w_out: bfloat16 [12288, 12288], P('head', 'seq'), may hold values from -0.0546875 to 0.0546875
- lengths: int32 [48], P('parts'), parts along dimension 0, may hold values from 1 to 4096, as said below
- key_cache: bfloat16 [48, 8, 4096, 128], P('parts', 'head', 'seq'), parts along dimension 0, may hold values from -600 to 600, as said below
- value_cache: bfloat16 [48, 8, 4096, 128], P('parts', 'head', 'seq'), parts along dimension 0, may hold values from -6 to 6
Outputs:
- attn_out: bfloat16 [48, 12288], P(('parts', 'head'), 'seq'), parts along dimension 0
There are 2 independent parts, one for each index of `parts`. A program takes and returns all parts, laid end to end along the dimension named above; an argument that names none is the same for every part. Nothing has to cross between parts.
Inputs may be any that keep to these rules, and one draw needn't show every extreme that they name: Sequence b holds lengths[b] cached tokens at positions 0 to lengths[b] - 1; its new token takes position lengths[b]. `key_cache`: positions at or past a sequence's length hold no data.
All inputs are finite; a program needn't handle non-finite values.
Results may differ from a plain program's by a relative error of at most 0.0075.
The roundings to bfloat16 on the way count: a program that leaves them out, or rounds other values in their place, can miss the bound.
Values may be sent and summed in bfloat16 or wider, within the bound.
No kernel may reach another device: no remote copies, remote signals or barrier semaphores. Data moves between devices by JAX's collectives and lax.ppermute only.
A program may use at most 64 MiB of HBM per device.

v0:
```python
import math

import jax
import jax.numpy as jnp
from jax import lax
from jax.sharding import PartitionSpec as P

D = 12288


EPSILON = 1e-05


def in_order(tiles, dim):
    tiles = jnp.moveaxis(tiles, 0, dim)
    dims = tiles.shape
    return tiles.reshape(*dims[:dim], dims[dim] * dims[dim + 1], *dims[dim + 2 :])


def sent_to_all(x, axis):
    copies = jnp.broadcast_to(x, (lax.axis_size(axis), *x.shape))
    return lax.all_to_all(copies, axis, split_axis=0, concat_axis=0, tiled=True)


def gather_directly(x, axis, dim):
    return in_order(sent_to_all(x, axis), dim)


def cut_along(x, dim, peers):
    before, after = (x.shape[:dim], x.shape[dim + 1 :])
    return jnp.moveaxis(x.reshape(*before, peers, -1, *after), dim, 0)


def summed_on_arrival(x, axis, dim):
    tiles = cut_along(x, dim, lax.axis_size(axis))
    arrived = lax.all_to_all(tiles, axis, split_axis=0, concat_axis=0, tiled=True)
    return arrived.sum(axis=0)


def in_one_piece(arrays, axis, dim, along):
    ends, at = ([], 0)
    for a in arrays[:-1]:
        at += a.shape[along]
        ends.append(at)
    both = jnp.concatenate(arrays, axis=along)
    return tuple(jnp.split(summed_on_arrival(both, axis, dim), ends, axis=along))


def in_one_piece_2(arrays, axis, dim, along):
    ends, at = ([], 0)
    for a in arrays[:-1]:
        at += a.shape[along]
        ends.append(at)
    both = jnp.concatenate(arrays, axis=along)
    return tuple(jnp.split(lax.all_gather(both, axis, axis=dim, tiled=True), ends, axis=along))


def side_by_side(arrays, axis, dim, along):
    widths = [math.prod(a.shape[along:]) for a in arrays]
    both = jnp.concatenate(
        [a.reshape(*a.shape[:along], w) for a, w in zip(arrays, widths)], axis=along
    )
    result = lax.all_gather(both, axis, axis=dim, tiled=True)
    tiles = jnp.split(result, [sum(widths[:k]) for k in range(1, len(widths))], axis=along)
    return tuple(
        (b.reshape(*result.shape[:along], *a.shape[along:]) for a, b in zip(arrays, tiles))
    )


def fold_blocks(totals, pieces):
    new_max = jnp.maximum(totals[0], jnp.max(pieces[0], axis=0))
    piece_factor = jnp.exp(pieces[0] - new_max[None])
    den_total = jnp.sum(piece_factor * pieces[1], axis=0)
    acc_total = jnp.sum(piece_factor[..., None] * pieces[2], axis=0)
    return (new_max, den_total, acc_total)


def local(hidden, norm_gain, w_query, w_key, w_value, w_out, lengths, key_cache, value_cache):
    batch_size, kv_local, block_len, head_size = key_cache.shape
    group_size = w_query.shape[1] // (kv_local * head_size)
    token_rows = gather_directly(hidden, "head", 0)
    widened = token_rows.astype(jnp.float32)
    square_local = jnp.sum(widened * widened, axis=1)
    scaled = (widened * norm_gain).astype(jnp.bfloat16)
    query_part = jnp.dot(scaled, w_query, preferred_element_type=jnp.float32)
    key_part = jnp.dot(scaled, w_key, preferred_element_type=jnp.float32)
    value_part = jnp.dot(scaled, w_value, preferred_element_type=jnp.float32)
    query_factor = float(head_size) ** (-0.5)
    square_tiled = jnp.broadcast_to(square_local[:, None], (batch_size, lax.axis_size("seq")))
    query_sum, key_sum, value_sum, norm_column = (
        summed_on_arrival(query_part, "seq", 1),
        *in_one_piece((key_part, value_part), "seq", 1, 0),
        summed_on_arrival(square_tiled, "seq", 1),
    )
    norm_total = norm_column[:, 0]
    inverse_rms = lax.rsqrt(norm_total / D + EPSILON)[:, None]
    queries = (query_sum * inverse_rms * query_factor).astype(jnp.bfloat16)
    new_keys = (key_sum * inverse_rms).astype(jnp.bfloat16)
    new_values = (value_sum * inverse_rms).astype(jnp.bfloat16)
    queries, new_keys, new_values = (
        lax.all_gather(queries, "seq", axis=1, tiled=True),
        *in_one_piece_2((new_keys, new_values), "seq", 1, 0),
    )
    grouped = queries.reshape(batch_size, kv_local, group_size, head_size)
    scores = jnp.einsum("bkgd,bkpd->bkgp", grouped, key_cache, preferred_element_type=jnp.float32)
    offset = lax.axis_index("seq") * block_len
    positions = offset + jnp.arange(block_len, dtype=jnp.int32)
    live_mask = (positions[None, :] < lengths[:, None])[:, None, None, :]
    block_max = jnp.max(jnp.where(live_mask, scores, -1e30), axis=-1)
    shifted = jnp.where(live_mask, scores - block_max[..., None], 0.0)
    weights = jnp.where(live_mask, jnp.exp(shifted), 0.0).astype(jnp.bfloat16)
    block_den = jnp.sum(weights.astype(jnp.float32), axis=-1)
    block_acc = jnp.einsum(
        "bkgp,bkpd->bkgd", weights, value_cache, preferred_element_type=jnp.float32
    )
    self_score = jnp.einsum(
        "oips,ois->oip",
        grouped,
        new_keys.reshape(batch_size, kv_local, head_size),
        preferred_element_type=jnp.float32,
    )
    initial = (
        jnp.full(block_max.shape, -1e30, jnp.float32),
        jnp.zeros(block_den.shape, jnp.float32),
        jnp.zeros(block_acc.shape, jnp.float32),
    )
    global_max, den_merged, acc_merged = fold_blocks(
        initial, side_by_side((block_max[None], block_den[None], block_acc[None]), "seq", 0, 4)
    )
    top_score = jnp.maximum(global_max, self_score)
    factors = jnp.exp(global_max - top_score)
    den_sum = den_merged * factors
    acc_sum = acc_merged * factors[..., None]
    own_weight = jnp.exp(self_score - top_score)
    denominator = den_sum + own_weight
    numerator = acc_sum + own_weight[..., None] * new_values.reshape(
        batch_size, kv_local, 1, head_size
    ).astype(jnp.float32)
    mixed = (
        (numerator / denominator[..., None])
        .astype(jnp.bfloat16)
        .reshape(batch_size, kv_local * group_size * head_size)
    )
    output = summed_on_arrival(jnp.dot(mixed, w_out, preferred_element_type=jnp.float32), "head", 0)
    return output.astype(jnp.bfloat16)


def solution(mesh):
    return jax.shard_map(
        local,
        mesh=mesh,
        in_specs=(
            P(("parts", "head"), "seq"),
            P("seq"),
            P("seq", "head"),
            P("seq", "head"),
            P("seq", "head"),
            P("head", "seq"),
            P("parts"),
            P("parts", "head", "seq", None),
            P("parts", "head", "seq", None),
        ),
        out_specs=P(("parts", "head"), "seq"),
        check_vma=False,
    )
```

profile of v0, /device:TPU:33, one launch (start us, length us, event | category | flops | bytes accessed | tf_op | source)
XLA Modules:
  0.0 357.4 jit_solution(9531133762320092091)
XLA Ops:
  6.5 0.0 copy-start
  6.6 0.0 copy-start.1
  6.6 1.4 broadcast_in_dim.49
  8.0 44.7 %all-to-all-start = ((bf16[8,3,384]{2,1,0:T(4,128)(2,1)}), bf16[8,3,384]{2,1,0:T(4,128)(2,1)S(1)}, u32[]{:S(2)}, u32[]{:S(2)}) async-start(bf16[8,3,384]{2,1,0:T(4,128)(2,1)} %broadcast_in_dim.49), calls=%async_computation | async-start | bytes 49152 | tf_op jit(solution)/shard_map/all_to_all | solution.py:22
  52.7 1.7 copy.66
  54.4 3.0 all-to-all-done
  57.4 0.8 multiply_reduce_fusion
  58.2 0.1 broadcast_in_dim.50
  58.3 0.6 transpose.24
  58.9 6.8 %all-to-all-start.2 = ((f32[32,24,1]{1,2,0:T(1,128)}), f32[32,24,1]{1,2,0:T(1,128)S(1)}, u32[]{:S(2)}, u32[]{:S(2)}) async-start(f32[32,24,1]{1,2,0:T(1,128)} %transpose.24), calls=%async_computation.2 | async-start | bytes 32768 | tf_op jit(solution)/shard_map/all_to_all | solution.py:36
  65.7 0.6 reshape.201
  66.3 0.0 copy-done.3
  66.3 1.6 convolution_bitcast_fusion
  67.8 1.1 reshape.206
  68.9 17.3 %all-to-all-done.2 = f32[32,24,1]{1,2,0:T(1,128)S(1)} async-done(((f32[32,24,1]{1,2,0:T(1,128)}), f32[32,24,1]{1,2,0:T(1,128)S(1)}, u32[]{:S(2)}, u32[]{:S(2)}) %all-to-all-start.2) | async-done | bytes 3104 | tf_op jit(solution)/shard_map/all_to_all | solution.py:36
  86.2 4.8 %all-to-all-start.1 = ((f32[32,1,1152]{2,1,0:T(1,128)}), f32[32,1,1152]{2,1,0:T(1,128)S(1)}, u32[]{:S(2)}, u32[]{:S(2)}) async-start(f32[32,1,1152]{2,1,0:T(1,128)} %reshape.206), calls=%async_computation.1 | async-start | bytes 294912 | tf_op jit(solution)/shard_map/all_to_all | solution.py:36
  91.0 0.1 all-gather.4.cloned.1.call-start
  91.1 0.7 broadcast_compare_fusion
  91.8 0.1 reduce_sum.74
  91.9 27.9 %all-to-all-done.1 = f32[32,1,1152]{2,1,0:T(1,128)S(1)} async-done(((f32[32,1,1152]{2,1,0:T(1,128)}), f32[32,1,1152]{2,1,0:T(1,128)S(1)}, u32[]{:S(2)}, u32[]{:S(2)}) %all-to-all-start.1) | async-done | bytes 147488 | tf_op jit(solution)/shard_map/all_to_all | solution.py:36
  119.8 0.5 broadcast.93
  120.3 1.0 reduce.10
  121.3 0.2 reshape.207
  121.6 0.1 fusion.13
  121.7 38.6 %all-gather = bf16[32,48,24]{1,2,0:T(8,128)(2,1)S(1)} all-gather(bf16[1,48,24]{1,2,0:T(8,128)(2,1)S(1)} %fusion.13), channel_id=1, replica_groups=mesh['parts'=2,'seq'=32,'head'=8] {'seq'}, dimensions={0}, use_global_device_ids=true | all-gather | bytes 76032 | tf_op jit(solution)/shard_map/all_gather | solution.py:101
  160.3 0.3 reshape.198
  160.5 0.1 reshape.190
  160.6 0.0 copy-done.1
  160.6 0.6 select_reduce_fusion
  161.2 0.2 convert_reduce_fusion
  161.5 0.0 copy-done.2
  161.5 0.4 convolution_bitcast_fusion.1
  161.9 0.3 copy.71
  162.1 0.3 copy.70
  162.4 0.3 pad_maximum_fusion
  162.7 0.9 copy.72
  163.6 0.1 all-gather.4.cloned.1.call-update
  163.6 0.0 copy-done.4
  163.6 1.0 fusion.14
  164.7 1.0 fusion.15
  165.8 0.1 copy.75
  165.9 0.1 reshape.208
  166.0 30.1 %all_to_all.25 = f32[32,1,192]{2,1,0:T(1,128)S(1)} all-to-all(f32[32,1,192]{2,1,0:T(1,128)S(1)} %reshape.208), channel_id=1, replica_groups=mesh['parts'=2,'seq'=32,'head'=8] {'seq'}, dimensions={0} | all-to-all | bytes 49152 | tf_op jit(solution)/shard_map/all_to_all | solution.py:36
  196.1 0.7 reduce.11
  196.8 0.1 reshape.209
  197.0 0.1 multiply_convert_fusion.6
  197.1 0.1 maximum_bitcast_fusion
  197.1 42.9 %all-gather.1 = bf16[32,4,48]{2,1,0:T(4,128)(2,1)S(1)} all-gather(bf16[1,4,48]{2,1,0:T(4,128)(2,1)S(1)} %maximum_bitcast_fusion), channel_id=1, replica_groups=mesh['parts'=2,'seq'=32,'head'=8] {'seq'}, dimensions={0}, use_global_device_ids=true | all-gather | bytes 12672 | tf_op jit(solution)/shard_map/all_gather | solution.py:55
  240.0 0.1 copy.76
  240.1 0.2 fusion.9
  240.3 0.1 copy.82
  240.4 61.3 %all-gather.4.cloned.1.call-done = f32[32,24,1,12,130]{4,1,3,2,0:T(8,128)} async-done(((f32[1,24,1,12,130]{4,1,3,2,0:T(8,128)}), f32[32,24,1,12,130]{4,1,3,2,0:T(8,128)}) %all-gather.4.cloned.1.call-update) | async-done | bytes 4792336 | tf_op jit(solution)/shard_map/all_gather | solution.py:63
  301.7 9.1 %fusion.18 = (f32[32,24,1,12,1]{4,1,3,2,0:T(8,128)}, f32[24,12]{0,1:T(8,128)S(1)}, f32[32,24,1,12,1]{4,1,3,2,0:T(8,128)}) fusion(f32[32,24,1,12,130]{4,1,3,2,0:T(8,128)} %all-gather.4.cloned.1.call-done), kind=kLoop, calls=%fused_computation.45 | loop fusion | flops 8928 | bytes 148608 | tf_op jit(solution)/shard_map/split | solution.py:64
  310.8 3.5 copy.88
  314.3 3.5 copy.87
  317.9 0.1 exponential_bitcast_fusion
  318.0 0.2 fusion.6
  318.2 0.2 copy.74
  318.4 5.1 %fusion = f32[24,12,128]{2,0,1:T(8,128)S(1)} fusion(f32[32,24,1,12,130]{4,1,3,2,0:T(8,128)} %all-gather.4.cloned.1.call-done, f32[32,24,12]{1,2,0:T(8,128)S(1)} %copy.74), kind=kLoop, calls=%fused_computation.1 | loop fusion | flops 2322432 | bytes 4902912 | tf_op jit(solution)/shard_map/reduce_sum | solution.py:74
  323.5 0.2 divide_convert_fusion
  323.7 0.0 copy-done
  323.7 0.3 fusion.1
  324.0 25.8 %all_to_all.26 = f32[8,3,384]{2,1,0:T(4,128)S(1)} all-to-all(f32[8,3,384]{2,1,0:T(4,128)S(1)} %copy.80), channel_id=1, replica_groups=mesh['parts'=2,'seq'=32,'head'=8] {'head'}, dimensions={0} | all-to-all | bytes 73728 | tf_op jit(solution)/shard_map/all_to_all | solution.py:36
  349.9 0.6 reduce_sum.79
  (16 shorter events, 0.3 us)
Async XLA Ops:
  6.5 317.2 %copy-start = (bf16[1536,384]{1,0:T(8,128)(2,1)S(1)}, bf16[1536,384]{1,0:T(8,128)(2,1)}, u32[]{:S(2)}) copy-start(bf16[1536,384]{1,0:T(8,128)(2,1)} %param.14) | copy-start | bytes 3538948
  6.6 154.1 %copy-start.1 = (bf16[24,1,128,128]{3,2,1,0:T(8,128)(2,1)S(1)}, bf16[24,1,128,128]{3,2,1,0:T(8,128)(2,1)}, u32[]{:S(2)}) copy-start(bf16[24,1,128,128]{3,2,1,0:T(8,128)(2,1)} %param.16) | copy-start | bytes 2359300
  8.0 49.4 %all-to-all-start = ((bf16[8,3,384]{2,1,0:T(4,128)(2,1)}), bf16[8,3,384]{2,1,0:T(4,128)(2,1)S(1)}, u32[]{:S(2)}, u32[]{:S(2)}) async-start(bf16[8,3,384]{2,1,0:T(4,128)(2,1)} %broadcast_in_dim.49), calls=%async_computation | async-start | bytes 49152 | tf_op jit(solution)/shard_map/all_to_all | solution.py:22
  57.4 8.9 %copy-start.3 = (bf16[8,3,384]{2,1,0:T(4,128)(2,1)}, bf16[8,3,384]{2,1,0:T(4,128)(2,1)S(1)}, u32[]{:S(2)}) copy-start(bf16[8,3,384]{2,1,0:T(4,128)(2,1)S(1)} %all-to-all-done) | copy-start | bytes 55300
  58.9 27.3 %all-to-all-start.2 = ((f32[32,24,1]{1,2,0:T(1,128)}), f32[32,24,1]{1,2,0:T(1,128)S(1)}, u32[]{:S(2)}, u32[]{:S(2)}) async-start(f32[32,24,1]{1,2,0:T(1,128)} %transpose.24), calls=%async_computation.2 | async-start | bytes 32768 | tf_op jit(solution)/shard_map/all_to_all | solution.py:36
  67.8 93.6 %copy-start.2 = (bf16[24,1,128,128]{3,2,1,0:T(8,128)(2,1)S(1)}, bf16[24,1,128,128]{3,2,1,0:T(8,128)(2,1)}, u32[]{:S(2)}) copy-start(bf16[24,1,128,128]{3,2,1,0:T(8,128)(2,1)} %param.17) | copy-start | bytes 2359300
  68.9 94.7 %copy-start.4 = (bf16[8,3,384]{2,1,0:T(4,128)(2,1)S(1)}, bf16[8,3,384]{2,1,0:T(4,128)(2,1)}, u32[]{:S(2)}) copy-start(bf16[8,3,384]{2,1,0:T(4,128)(2,1)} %copy-done.3) | copy-start | bytes 55300
  86.2 33.6 %all-to-all-start.1 = ((f32[32,1,1152]{2,1,0:T(1,128)}), f32[32,1,1152]{2,1,0:T(1,128)S(1)}, u32[]{:S(2)}, u32[]{:S(2)}) async-start(f32[32,1,1152]{2,1,0:T(1,128)} %reshape.206), calls=%async_computation.1 | async-start | bytes 294912 | tf_op jit(solution)/shard_map/all_to_all | solution.py:36
  91.0 210.7 %all-gather.4.cloned.1.call-start = ((), (), s32[]{:S(2)}) async-start(), calls=%async_computation.5 | async-start | bytes 9732096 | tf_op jit(solution)/shard_map/all_gather | solution.py:63
Sparse Core Ops, SparseCore 0:
  163.7 137.9 all-gather.3
where the time goes:
time: 358 us; the launch traced here: 357 us
  blocking collectives  137 us (38%)
  waiting for transfers between devices  110 us (31%)
  starting transfers between devices  56.3 us (16%)
  other arithmetic  19.4 us (5%)
  local copies, waits for them, and re-layouts  15.8 us (4%)
  between operations  13.7 us (4%)
  matrix products  5.05 us (1%)
    all_gather x1, waiting for transfers between devices, side_by_side(): result = lax.all_gather(both, axis, axis=dim, tiled=True)  61.3 us
    all_to_all x2, blocking collectives, summed_on_arrival(): lax.all_to_all(tiles, axis, split_axis=0, concat_axis=0, tiled=True)  56 us
    all_to_all x2, waiting for transfers between devices, summed_on_arrival(): lax.all_to_all(tiles, axis, split_axis=0, concat_axis=0, tiled=True)  45.3 us
    all_to_all x1, starting transfers between devices, sent_to_all(): return lax.all_to_all(copies, axis, split_axis=0, concat_axis=0, tiled=True)  44.7 us
    all_gather x1, blocking collectives, in_one_piece_2(): lax.all_gather(both, axis, axis=dim, tiled=True)  42.9 us
    all_gather x1, blocking collectives, local(): lax.all_gather(queries, 'seq', axis=1, tiled=True)  38.6 us
    all_to_all x2, starting transfers between devices, summed_on_arrival(): lax.all_to_all(tiles, axis, split_axis=0, concat_axis=0, tiled=True)  11.5 us
    unnamed x19, local copies, waits for them, and re-layouts  10.6 us
  transfers between devices with their start and end apart: 4, of which 4 were waited for; matrix products, arithmetic and copies ran while one was open for 3% of the time, Pallas kernels for 0%

commit v1 on v0

v1 whole, which is shorter than its diff:
```python
import jax
import jax.numpy as jnp
from jax import lax
from jax.sharding import PartitionSpec as P

D = 12288
EPSILON = 1e-05


def exchange(x, axis):
    return lax.all_to_all(x, axis, split_axis=0, concat_axis=0, tiled=True)


def sent_to_all(x, axis):
    return exchange(jnp.broadcast_to(x, (lax.axis_size(axis), *x.shape)), axis)


def padded(x, rows):
    return jnp.pad(x, ((0, rows - x.shape[0]),) + ((0, 0),) * (x.ndim - 1))


def lane_row(x, lanes):
    return jnp.pad(x, ((0, 0), (0, lanes - x.shape[1])))[:, None, :]


def local(hidden, norm_gain, w_query, w_key, w_value, w_out, lengths, key_cache, value_cache):
    batch, _, block_len, hd = key_cache.shape
    group = w_query.shape[1] // hd
    peers = lax.axis_size("seq")
    me = lax.axis_index("seq")
    slots = group + 2
    half = batch // 2

    tokens = sent_to_all(hidden, "head").reshape(batch, hidden.shape[1])
    widened = tokens.astype(jnp.float32)
    squares = jnp.sum(widened * widened, axis=1)
    scaled = (widened * norm_gain).astype(jnp.bfloat16)

    def project(w):
        return jnp.dot(scaled, w, preferred_element_type=jnp.float32)

    q_part = project(w_query).reshape(batch, group, hd).transpose(1, 0, 2)
    parts = jnp.concatenate([q_part, project(w_key)[None], project(w_value)[None]], axis=0)
    parts = padded(parts.reshape(2 * slots, half, hd), peers)
    sq_rows = lane_row(jnp.tile(squares.reshape(2, half), (peers // 2, 1)), hd)
    sent = jnp.concatenate([parts, sq_rows], axis=1).reshape(peers, 1, (half + 1) * hd)
    total = exchange(sent, "seq").reshape(peers, half + 1, hd).sum(axis=0)
    inverse_rms = lax.rsqrt(total[half, :half] / D + EPSILON)[:, None]
    factor = jnp.where(me < 2 * group, jnp.float32(float(hd) ** -0.5), jnp.float32(1.0))
    rounded = (total[:half] * inverse_rms * factor).astype(jnp.bfloat16)
    rows = sent_to_all(rounded.reshape(1, half * hd), "seq").reshape(peers, half, hd)
    rows = rows[: 2 * slots].reshape(slots, batch, hd)
    queries = rows[:group].transpose(1, 0, 2)
    new_keys, new_values = rows[group], rows[group + 1]

    scores = jnp.einsum("bgd,bpd->bgp", queries, key_cache[:, 0], preferred_element_type=jnp.float32)
    positions = me * block_len + jnp.arange(block_len, dtype=jnp.int32)
    live = (positions[None, :] < lengths[:, None])[:, None, :]
    block_max = jnp.max(jnp.where(live, scores, -1e30), axis=-1)
    shifted = jnp.where(live, scores - block_max[..., None], 0.0)
    weights = jnp.where(live, jnp.exp(shifted), 0.0).astype(jnp.bfloat16)
    block_den = jnp.sum(weights.astype(jnp.float32), axis=-1)
    block_acc = jnp.einsum(
        "bgp,bpd->bgd", weights, value_cache[:, 0], preferred_element_type=jnp.float32
    )
    self_score = jnp.einsum("bgd,bd->bg", queries, new_keys, preferred_element_type=jnp.float32)
    self_score = jnp.where(me == 0, self_score, -1e30)
    top = jnp.maximum(block_max, self_score)
    keep = jnp.exp(block_max - top)
    own = jnp.where(me == 0, jnp.exp(self_score - top), 0.0)
    den = keep * block_den + own
    acc = keep[..., None] * block_acc + own[..., None] * new_values[:, None, :].astype(jnp.float32)

    share = batch * group // peers
    acc = acc.transpose(1, 0, 2).reshape(peers, share, hd)
    stats = jnp.concatenate([top.T.reshape(peers, share), den.T.reshape(peers, share)], axis=1)
    sent = jnp.concatenate([acc, lane_row(stats, hd)], axis=1).reshape(peers, 1, (share + 1) * hd)
    blocks = exchange(sent, "seq").reshape(peers, share + 1, hd)
    tops, dens = blocks[:, share, :share], blocks[:, share, share : 2 * share]
    factors = jnp.exp(tops - jnp.max(tops, axis=0))
    denominator = jnp.sum(factors * dens, axis=0)
    numerator = jnp.sum(factors[..., None] * blocks[:, :share], axis=0)
    mixed = (numerator / denominator[:, None]).astype(jnp.bfloat16)
    mixed = sent_to_all(mixed.reshape(1, share * hd), "seq").reshape(group, batch, hd)

    out = jnp.einsum(
        "gbd,gdn->bn", mixed, w_out.reshape(group, hd, -1), preferred_element_type=jnp.float32
    )
    ways = lax.axis_size("head")
    return exchange(out.reshape(ways, batch // ways, -1), "head").sum(axis=0).astype(jnp.bfloat16)


def solution(mesh):
    return jax.shard_map(
        local,
        mesh=mesh,
        in_specs=(
            P(("parts", "head"), "seq"),
            P("seq"),
            P("seq", "head"),
            P("seq", "head"),
            P("seq", "head"),
            P("head", "seq"),
            P("parts"),
            P("parts", "head", "seq", None),
            P("parts", "head", "seq", None),
        ),
        out_specs=P(("parts", "head"), "seq"),
        check_vma=False,
    )
```

time: 358 us -> 211 us (0.59)
  blocking collectives: 137 us -> 76.2 us
  waiting for transfers between devices: 110 us -> 63.3 us
  other arithmetic: 19.4 us -> 4.79 us
  between operations: 13.7 us -> 0.3 us
  local copies, waits for them, and re-layouts: 15.8 us -> 7.3 us
    all_gather x2 -> x0, blocking collectives: 81.5 us -> none  [the longest x1 42.9 us: in_one_piece_2(): lax.all_gather(both, axis, axis=dim, tiled=True)]
    all_gather x1 -> x0, waiting for transfers between devices: 61.3 us -> none  [side_by_side(): result = lax.all_gather(both, axis, axis=dim, tiled=True)]
    all_to_all x2 -> x3, blocking collectives: 56 us -> 76.2 us  [exchange(): return lax.all_to_all(x, axis, split_axis=0, concat_axis=0, tiled=True)]
    all_to_all x3, waiting for transfers between devices: 48.3 us -> 63.3 us  [exchange(): return lax.all_to_all(x, axis, split_axis=0, concat_axis=0, tiled=True)]
    split x1 -> x0, other arithmetic: 9.09 us -> none  [side_by_side(): jnp.split(result, [sum(widths[:k]) for k in range(1, len(widths))], axis=...]
    unnamed x19, local copies, waits for them, and re-layouts: 10.6 us -> 2.79 us
    reduce_sum x7 -> x5, other arithmetic: 6.81 us -> 1 us  [the longest x1 0.6 us: local(): exchange(out.reshape(ways, batch // ways, -1), 'head').sum(axis=0)]
  transfers between devices with their start and end apart: 4 -> 3, of which waited for: 4 -> 3; matrix products, arithmetic and copies ran while one was open for 3% -> 1% of each run, Pallas kernels for 0% -> 0%
where the time goes in v1:
time: 211 us; the launch traced here: 210 us
  blocking collectives  76.2 us (36%)
  waiting for transfers between devices  63.3 us (30%)
  starting transfers between devices  56.3 us (27%)
  local copies, waits for them, and re-layouts  7.3 us (3%)
  other arithmetic  4.79 us (2%)
  matrix products  2.19 us (1%)
    all_to_all x3, blocking collectives, exchange(): return lax.all_to_all(x, axis, split_axis=0, concat_axis=0, tiled=True)  76.2 us
    all_to_all x3, waiting for transfers between devices, exchange(): return lax.all_to_all(x, axis, split_axis=0, concat_axis=0, tiled=True)  63.3 us
    all_to_all x3, starting transfers between devices, exchange(): return lax.all_to_all(x, axis, split_axis=0, concat_axis=0, tiled=True)  56.3 us
  transfers between devices with their start and end apart: 3, of which 3 were waited for; matrix products, arithmetic and copies ran while one was open for 1% of the time, Pallas kernels for 0%

profile of v1, /device:TPU:33, one launch (start us, length us, event | category | flops | bytes accessed | tf_op | source)
XLA Modules:
  0.0 210.5 jit_solution(15809396111851025124)
XLA Ops:
  0.0 0.0 copy-start
  0.0 1.4 broadcast_in_dim.62
  1.4 44.7 %all-to-all-start = ((bf16[8,3,384]{2,1,0:T(4,128)(2,1)}), bf16[8,3,384]{2,1,0:T(4,128)(2,1)S(1)}, u32[]{:S(2)}, u32[]{:S(2)}) async-start(bf16[8,3,384]{2,1,0:T(4,128)(2,1)} %broadcast_in_dim.62), calls=%async_computation | async-start | bytes 49152 | tf_op jit(solution)/shard_map/all_to_all | solution.py:11
  46.1 0.0 copy-start.5
  46.1 0.0 copy-start.3
  46.1 0.0 copy-start.4
  46.1 1.7 copy.30
  47.8 3.0 %all-to-all-done = bf16[8,3,384]{2,1,0:T(4,128)(2,1)S(1)} async-done(((bf16[8,3,384]{2,1,0:T(4,128)(2,1)}), bf16[8,3,384]{2,1,0:T(4,128)(2,1)S(1)}, u32[]{:S(2)}, u32[]{:S(2)}) %all-to-all-start) | async-done | bytes 18464 | tf_op jit(solution)/shard_map/all_to_all | solution.py:11
  50.8 0.0 copy-done.5
  50.8 0.1 multiply_reduce_fusion
  51.0 0.0 copy-done.3
  51.0 0.1 convolution_bitcast_fusion.3
  51.1 0.0 copy-done.4
  51.1 0.1 convolution_bitcast_fusion.4
  51.3 0.5 convolution_bitcast_fusion.1
  51.8 0.1 tile.10
  51.9 0.0 copy-start.6
  52.0 0.9 reshape.165
  52.9 0.0 copy-start.1
  52.9 6.9 %all-to-all-start.1 = ((f32[32,1,1664]{2,1,0:T(1,128)}), f32[32,1,1664]{2,1,0:T(1,128)S(1)}, u32[]{:S(2)}, u32[]{:S(2)}) async-start(f32[32,1,1664]{2,1,0:T(1,128)} %reshape.165), calls=%async_computation.1 | async-start | bytes 425984 | tf_op jit(solution)/shard_map/all_to_all | solution.py:11
  59.8 36.2 %all-to-all-done.1 = f32[32,1,1664]{2,1,0:T(1,128)S(1)} async-done(((f32[32,1,1664]{2,1,0:T(1,128)}), f32[32,1,1664]{2,1,0:T(1,128)S(1)}, u32[]{:S(2)}, u32[]{:S(2)}) %all-to-all-start.1) | async-done | bytes 213024 | tf_op jit(solution)/shard_map/all_to_all | solution.py:11
  96.0 0.1 reduce_sum.59
  96.1 0.1 fusion.19
  96.2 0.1 broadcast_in_dim.66
  96.3 0.5 broadcast.98
  96.8 1.2 reduce.7
  98.0 0.6 reshape.171
  98.7 4.8 %all-to-all-start.2 = ((bf16[32,2,768]{2,1,0:T(2,128)(2,1)}), bf16[32,2,768]{2,1,0:T(2,128)(2,1)S(1)}, u32[]{:S(2)}, u32[]{:S(2)}) async-start(bf16[32,2,768]{2,1,0:T(2,128)(2,1)} %reshape.171), calls=%async_computation.2 | async-start | bytes 196608 | tf_op jit(solution)/shard_map/all_to_all | solution.py:11
  103.4 0.0 copy-start.2
  103.5 0.0 copy-done.6
  103.5 0.1 broadcast_compare_fusion
  103.6 24.2 %all-to-all-done.2 = bf16[32,2,768]{2,1,0:T(2,128)(2,1)S(1)} async-done(((bf16[32,2,768]{2,1,0:T(2,128)(2,1)}), bf16[32,2,768]{2,1,0:T(2,128)(2,1)S(1)}, u32[]{:S(2)}, u32[]{:S(2)}) %all-to-all-start.2) | async-done | bytes 98336 | tf_op jit(solution)/shard_map/all_to_all | solution.py:11
  127.7 0.1 reshape.172
  127.8 0.4 slice_reduce_fusion
  128.3 0.1 slice.47
  128.4 0.1 fusion.6
  128.5 0.0 copy-done.1
  128.5 0.6 select_reduce_fusion
  129.1 0.2 convert_reduce_fusion
  129.4 0.0 copy-done.2
  129.4 0.4 fusion.1
  129.8 0.1 copy.33
  129.9 0.1 copy.34
  130.0 0.1 reshape.151
  130.1 0.1 copy.35
  130.1 0.1 reshape.152
  130.2 0.1 select_maximum_fusion.1
  130.3 0.2 reshape.167
  130.5 35.7 %all_to_all.30 = f32[32,1,1280]{2,1,0:T(1,128)S(1)} all-to-all(f32[32,1,1280]{2,1,0:T(1,128)S(1)} %reshape.167), channel_id=1, replica_groups=mesh['parts'=2,'seq'=32,'head'=8] {'seq'}, dimensions={0} | all-to-all | bytes 327680 | tf_op jit(solution)/shard_map/all_to_all | solution.py:11
  166.2 0.4 reduce.4
  166.7 0.1 fusion.26
  166.8 0.1 fusion.5
  167.0 0.1 fusion.20
  167.0 0.1 broadcast_in_dim.72
  167.1 1.1 reduce.8
  168.2 0.1 reshape.173
  168.3 28.7 %all_to_all.31 = bf16[32,2,576]{2,1,0:T(2,128)(2,1)S(1)} all-to-all(bf16[32,2,576]{2,1,0:T(2,128)(2,1)S(1)} %reshape.173), channel_id=1, replica_groups=mesh['parts'=2,'seq'=32,'head'=8] {'seq'}, dimensions={0} | all-to-all | bytes 147456 | tf_op jit(solution)/shard_map/all_to_all | solution.py:11
  197.1 0.1 reshape.174
  197.2 0.4 reduce.5
  197.6 0.1 reshape.155
  197.8 0.0 copy-done
  197.8 0.3 convolution_bitcast_fusion.2
  198.1 11.8 %all_to_all.32 = f32[8,3,384]{2,1,0:T(4,128)S(1)} all-to-all(f32[8,3,384]{2,1,0:T(4,128)S(1)} %copy.39), channel_id=1, replica_groups=mesh['parts'=2,'seq'=32,'head'=8] {'head'}, dimensions={0} | all-to-all | bytes 73728 | tf_op jit(solution)/shard_map/all_to_all | solution.py:11
  209.9 0.6 reduce_sum.65
  (18 shorter events, 0.4 us)
Async XLA Ops:
  0.0 197.8 %copy-start = (bf16[1536,384]{1,0:T(8,128)(2,1)S(1)}, bf16[1536,384]{1,0:T(8,128)(2,1)}, u32[]{:S(2)}) copy-start(bf16[1536,384]{1,0:T(8,128)(2,1)} %param.14) | copy-start | bytes 3538948
  1.4 49.4 %all-to-all-start = ((bf16[8,3,384]{2,1,0:T(4,128)(2,1)}), bf16[8,3,384]{2,1,0:T(4,128)(2,1)S(1)}, u32[]{:S(2)}, u32[]{:S(2)}) async-start(bf16[8,3,384]{2,1,0:T(4,128)(2,1)} %broadcast_in_dim.62), calls=%async_computation | async-start | bytes 49152 | tf_op jit(solution)/shard_map/all_to_all | solution.py:11
  46.1 4.7 %copy-start.5 = (f32[384]{0:T(512)S(1)}, f32[384]{0:T(512)}, u32[]{:S(2)}) copy-start(f32[384]{0:T(512)} %param.10) | copy-start | bytes 4612
  46.1 4.9 %copy-start.3 = (bf16[384,128]{1,0:T(8,128)(2,1)S(1)}, bf16[384,128]{1,0:T(8,128)(2,1)}, u32[]{:S(2)}) copy-start(bf16[384,128]{1,0:T(8,128)(2,1)} %param.13) | copy-start | bytes 294916
  46.1 5.0 %copy-start.4 = (bf16[384,128]{1,0:T(8,128)(2,1)S(1)}, bf16[384,128]{1,0:T(8,128)(2,1)}, u32[]{:S(2)}) copy-start(bf16[384,128]{1,0:T(8,128)(2,1)} %param.12) | copy-start | bytes 294916
  51.9 51.5 %copy-start.6 = (s32[24]{0:T(128)S(1)}, s32[24]{0:T(128)}, u32[]{:S(2)}) copy-start(s32[24]{0:T(128)} %param.15) | copy-start | bytes 292
  52.9 75.7 %copy-start.1 = (bf16[24,1,128,128]{3,2,1,0:T(8,128)(2,1)S(1)}, bf16[24,1,128,128]{3,2,1,0:T(8,128)(2,1)}, u32[]{:S(2)}) copy-start(bf16[24,1,128,128]{3,2,1,0:T(8,128)(2,1)} %param.16) | copy-start | bytes 2359300
  52.9 43.1 %all-to-all-start.1 = ((f32[32,1,1664]{2,1,0:T(1,128)}), f32[32,1,1664]{2,1,0:T(1,128)S(1)}, u32[]{:S(2)}, u32[]{:S(2)}) async-start(f32[32,1,1664]{2,1,0:T(1,128)} %reshape.165), calls=%async_computation.1 | async-start | bytes 425984 | tf_op jit(solution)/shard_map/all_to_all | solution.py:11
  98.7 29.1 %all-to-all-start.2 = ((bf16[32,2,768]{2,1,0:T(2,128)(2,1)}), bf16[32,2,768]{2,1,0:T(2,128)(2,1)S(1)}, u32[]{:S(2)}, u32[]{:S(2)}) async-start(bf16[32,2,768]{2,1,0:T(2,128)(2,1)} %reshape.171), calls=%async_computation.2 | async-start | bytes 196608 | tf_op jit(solution)/shard_map/all_to_all | solution.py:11
  103.4 26.0 %copy-start.2 = (bf16[24,1,128,128]{3,2,1,0:T(8,128)(2,1)S(1)}, bf16[24,1,128,128]{3,2,1,0:T(8,128)(2,1)}, u32[]{:S(2)}) copy-start(bf16[24,1,128,128]{3,2,1,0:T(8,128)(2,1)} %param.17) | copy-start | bytes 2359300

commit v2 on v1

v2 whole, which is shorter than its diff:
```python
import jax
import jax.numpy as jnp
from jax import lax
from jax.sharding import PartitionSpec as P

D = 12288
EPSILON = 1e-05
NEAR = 4


def near_groups():
    peers = lax.axis_size("seq")
    return [[first + i for i in range(NEAR)] for first in range(0, peers, NEAR)]


def far_groups():
    peers = lax.axis_size("seq")
    return [list(range(first, peers, NEAR)) for first in range(NEAR)]


def exchange(x, axis, groups=None):
    return lax.all_to_all(
        x, axis, split_axis=0, concat_axis=0, tiled=True, axis_index_groups=groups
    )


def sent_to_all(x, axis, groups=None):
    ways = lax.axis_size(axis) if groups is None else len(groups[0])
    return exchange(jnp.broadcast_to(x, (ways, *x.shape)), axis, groups)


def to_rows(x, rows, lanes):
    return jnp.pad(x, ((0, 0), (0, rows - x.shape[1]), (0, lanes - x.shape[2])))


def fold(tops, dens, accs):
    top = jnp.max(tops, axis=0)
    factors = jnp.exp(tops - top)
    return top, jnp.sum(factors * dens, axis=0), jnp.sum(factors[..., None] * accs, axis=0)


def packed(top, den, acc):
    n, heads, batch, hd = acc.shape
    stats = jnp.concatenate([top, den], axis=1)
    return jnp.concatenate([acc.reshape(n, heads * batch, hd), to_rows(stats, 8, hd)], axis=1)


def unpacked(x, heads, batch):
    n, _, hd = x.shape
    acc = x[:, : heads * batch].reshape(n, heads, batch, hd)
    stats = x[:, heads * batch :, :batch]
    return stats[:, :heads], stats[:, heads : 2 * heads], acc


def local(hidden, norm_gain, w_query, w_key, w_value, w_out, lengths, key_cache, value_cache):
    batch, _, block_len, hd = key_cache.shape
    group = w_query.shape[1] // hd
    me = lax.axis_index("seq")
    near, far = near_groups(), far_groups()
    heads = group // NEAR
    piece = 2 * batch // NEAR
    main = heads * batch
    rows = main + piece + 4

    tokens = sent_to_all(hidden, "head").reshape(batch, hidden.shape[1])
    widened = tokens.astype(jnp.float32)
    squares = jnp.sum(widened * widened, axis=1)
    scaled = (widened * norm_gain).astype(jnp.bfloat16)

    def project(w):
        return jnp.dot(scaled, w, preferred_element_type=jnp.float32)

    q_part = project(w_query).reshape(batch, group, hd).transpose(1, 0, 2)
    kv_part = jnp.concatenate([project(w_key), project(w_value)], axis=0)
    sq_row = jnp.broadcast_to(squares, (NEAR, 1, batch))
    sent = jnp.concatenate(
        [q_part.reshape(NEAR, main, hd), kv_part.reshape(NEAR, piece, hd), to_rows(sq_row, 4, hd)],
        axis=1,
    )
    quarter = exchange(sent, "seq", near).sum(axis=0)
    total = sent_to_all(quarter, "seq", far).sum(axis=0)
    inverse_rms = lax.rsqrt(total[main + piece, :batch] / D + EPSILON)
    mine = lax.rem(me, NEAR)
    halves = inverse_rms.reshape(2, piece)
    kv_rms = jnp.where(lax.rem(mine, 2) == 0, halves[0], halves[1])
    queries = total[:main].reshape(heads, batch, hd) * inverse_rms[:, None] * float(hd) ** -0.5
    new_kv = total[main : main + piece] * kv_rms[:, None]
    rounded = jnp.concatenate(
        [queries.reshape(main, hd).astype(jnp.bfloat16), new_kv.astype(jnp.bfloat16)], axis=0
    )
    rounded = jnp.pad(rounded, ((0, rows - rounded.shape[0]), (0, 0)))
    gathered = sent_to_all(rounded, "seq", near)
    queries = gathered[:, :main].reshape(group, batch, hd).transpose(1, 0, 2)
    new_kv = gathered[:, main : main + piece].reshape(2, batch, hd)
    new_keys, new_values = new_kv[0], new_kv[1]

    scores = jnp.einsum("bgd,bpd->bgp", queries, key_cache[:, 0], preferred_element_type=jnp.float32)
    positions = me * block_len + jnp.arange(block_len, dtype=jnp.int32)
    live = (positions[None, :] < lengths[:, None])[:, None, :]
    block_max = jnp.max(jnp.where(live, scores, -1e30), axis=-1)
    shifted = jnp.where(live, scores - block_max[..., None], 0.0)
    weights = jnp.where(live, jnp.exp(shifted), 0.0).astype(jnp.bfloat16)
    block_den = jnp.sum(weights.astype(jnp.float32), axis=-1)
    block_acc = jnp.einsum(
        "bgp,bpd->bgd", weights, value_cache[:, 0], preferred_element_type=jnp.float32
    )
    self_score = jnp.einsum("bgd,bd->bg", queries, new_keys, preferred_element_type=jnp.float32)
    self_score = jnp.where(me == 0, self_score, -1e30)
    top = jnp.maximum(block_max, self_score)
    keep = jnp.exp(block_max - top)
    own = jnp.where(me == 0, jnp.exp(self_score - top), 0.0)
    den = keep * block_den + own
    acc = keep[..., None] * block_acc + own[..., None] * new_values[:, None, :].astype(jnp.float32)

    split = (NEAR, heads, batch)
    sent = packed(
        top.T.reshape(split), den.T.reshape(split), acc.transpose(1, 0, 2).reshape(*split, hd)
    )
    top, den, acc = fold(*unpacked(exchange(sent, "seq", near), heads, batch))
    quarter = packed(top[None], den[None], acc[None])[0]
    _, den, acc = fold(*unpacked(sent_to_all(quarter, "seq", far), heads, batch))
    mixed = (acc / den[..., None]).astype(jnp.bfloat16).reshape(main, hd)
    mixed = sent_to_all(mixed, "seq", near).reshape(group, batch, hd)

    out = jnp.einsum(
        "gbd,gdn->bn", mixed, w_out.reshape(group, hd, -1), preferred_element_type=jnp.float32
    )
    ways = lax.axis_size("head")
    return exchange(out.reshape(ways, batch // ways, -1), "head").sum(axis=0).astype(jnp.bfloat16)


def solution(mesh):
    return jax.shard_map(
        local,
        mesh=mesh,
        in_specs=(
            P(("parts", "head"), "seq"),
            P("seq"),
            P("seq", "head"),
            P("seq", "head"),
            P("seq", "head"),
            P("head", "seq"),
            P("parts"),
            P("parts", "head", "seq", None),
            P("parts", "head", "seq", None),
        ),
        out_specs=P(("parts", "head"), "seq"),
        check_vma=False,
    )
```

time: 211 us -> 206 us (0.976)
  waiting for transfers between devices: 63.3 us -> 45.5 us
  blocking collectives: 76.2 us -> 89.8 us
  starting transfers between devices: 56.3 us -> 60.8 us
  other arithmetic: 4.79 us -> 1.81 us
    all_to_all x3, waiting for transfers between devices: 63.3 us -> 45.5 us  [exchange(): lax.all_to_all(x, axis, split_axis=0, concat_axis=0, tiled=True, axis_ind...]
    all_to_all x3 -> x5, blocking collectives: 76.2 us -> 89.8 us  [exchange(): lax.all_to_all(x, axis, split_axis=0, concat_axis=0, tiled=True, axis_ind...]
    all_to_all x3, starting transfers between devices: 56.3 us -> 60.8 us  [exchange(): lax.all_to_all(x, axis, split_axis=0, concat_axis=0, tiled=True, axis_ind...]
    broadcast_in_dim x2 -> x0, other arithmetic: 2.26 us -> none  [sent_to_all(): return exchange(jnp.broadcast_to(x, (lax.axis_size(axis), *x.shape)), axis)]
where the time goes in v2:
time: 206 us
  blocking collectives  89.8 us (44%)
  starting transfers between devices  60.8 us (30%)
  waiting for transfers between devices  45.5 us (22%)
  local copies, waits for them, and re-layouts  5.4 us (3%)
  matrix products  2.18 us (1%)
    all_to_all x5, blocking collectives, exchange(): lax.all_to_all(x, axis, split_axis=0, concat_axis=0, tiled=True, axis_ind...  89.8 us
    all_to_all x3, starting transfers between devices, exchange(): lax.all_to_all(x, axis, split_axis=0, concat_axis=0, tiled=True, axis_ind...  60.8 us
    all_to_all x3, waiting for transfers between devices, exchange(): lax.all_to_all(x, axis, split_axis=0, concat_axis=0, tiled=True, axis_ind...  45.5 us
  transfers between devices with their start and end apart: 3, of which 3 were waited for; matrix products, arithmetic and copies ran while one was open for 1% of the time, Pallas kernels for 0%

profile of v2, /device:TPU:33, one launch (start us, length us, event | category | flops | bytes accessed | tf_op | source)
XLA Modules:
  0.0 205.7 jit_solution(8474164264885546322)
XLA Ops:
  0.0 0.0 copy-start
  0.0 1.4 broadcast_in_dim.67
  1.4 44.7 %all-to-all-start = ((bf16[8,3,384]{2,1,0:T(4,128)(2,1)}), bf16[8,3,384]{2,1,0:T(4,128)(2,1)S(1)}, u32[]{:S(2)}, u32[]{:S(2)}) async-start(bf16[8,3,384]{2,1,0:T(4,128)(2,1)} %broadcast_in_dim.67), calls=%async_computation | async-start | bytes 49152 | tf_op jit(solution)/shard_map/all_to_all | solution.py:22
  46.1 0.0 copy-start.3
  46.1 0.0 copy-start.5
  46.1 0.0 copy-start.4
  46.1 1.7 copy.26
  47.8 3.0 %all-to-all-done = bf16[8,3,384]{2,1,0:T(4,128)(2,1)S(1)} async-done(((bf16[8,3,384]{2,1,0:T(4,128)(2,1)}), bf16[8,3,384]{2,1,0:T(4,128)(2,1)S(1)}, u32[]{:S(2)}, u32[]{:S(2)}) %all-to-all-start) | async-done | bytes 18464 | tf_op jit(solution)/shard_map/all_to_all | solution.py:22
  50.8 0.0 copy-done.3
  50.8 0.0 copy-done.5
  50.9 0.1 fusion.25
  51.0 0.0 copy-done.4
  51.0 0.1 fusion.26
  51.1 0.1 multiply_convert_fusion
  51.3 0.1 broadcast_in_dim.68
  51.4 0.5 fusion.32
  51.9 8.0 %all_to_all.40 = f32[4,88,128]{2,1,0:T(8,128)S(1)} all-to-all(f32[4,88,128]{2,1,0:T(8,128)S(1)} %pad_maximum_fusion), channel_id=1, replica_groups={{0,8,16,24},{32,40,48,56},{64,72,80,88},{96,104,112,120},{128,136,144,1..., dimensions={0} | all-to-all | bytes 360448 | tf_op jit(solution)/shard_map/all_to_all | solution.py:22
  60.0 0.0 copy-start.6
  60.0 0.0 copy-start.1
  60.0 0.8 broadcast_in_dim.69
  60.7 7.3 %all-to-all-start.2 = ((f32[8,88,128]{2,1,0:T(8,128)}), f32[8,88,128]{2,1,0:T(8,128)S(1)}, u32[]{:S(2)}, u32[]{:S(2)}) async-start(f32[8,88,128]{2,1,0:T(8,128)} %broadcast_in_dim.69), calls=%async_computation.2 | async-start | bytes 720896 | tf_op jit(solution)/shard_map/all_to_all | solution.py:22
  68.1 37.9 %all-to-all-done.2 = f32[8,88,128]{2,1,0:T(8,128)S(1)} async-done(((f32[8,88,128]{2,1,0:T(8,128)}), f32[8,88,128]{2,1,0:T(8,128)S(1)}, u32[]{:S(2)}, u32[]{:S(2)}) %all-to-all-start.2) | async-done | bytes 360480 | tf_op jit(solution)/shard_map/all_to_all | solution.py:22
  106.0 0.0 copy-start.2
  106.0 0.1 fusion.27
  106.1 0.1 fusion.24
  106.2 0.1 mul.110
  106.3 0.1 fusion.16
  106.4 0.6 broadcast_in_dim.70
  107.0 8.8 %all-to-all-start.3 = ((bf16[4,88,128]{2,1,0:T(8,128)(2,1)}), bf16[4,88,128]{2,1,0:T(8,128)(2,1)S(1)}, u32[]{:S(2)}, u32[]{:S(2)}) async-start(bf16[4,88,128]{2,1,0:T(8,128)(2,1)} %broadcast_in_dim.70), calls=%async_computation.3 | async-start | bytes 180224 | tf_op jit(solution)/shard_map/all_to_all | solution.py:22
  115.8 0.0 copy-done.6
  115.8 0.1 broadcast_compare_fusion
  115.9 4.6 %all-to-all-done.3 = bf16[4,88,128]{2,1,0:T(8,128)(2,1)S(1)} async-done(((bf16[4,88,128]{2,1,0:T(8,128)(2,1)}), bf16[4,88,128]{2,1,0:T(8,128)(2,1)S(1)}, u32[]{:S(2)}, u32[]{:S(2)}) %all-to-all-start.3) | async-done | bytes 90144 | tf_op jit(solution)/shard_map/all_to_all | solution.py:22
  120.5 0.1 fusion.7
  120.6 0.0 copy-done.1
  120.7 0.6 select_reduce_fusion
  121.2 0.2 convert_reduce_fusion
  121.5 0.0 copy-done.2
  121.5 0.4 fusion.1
  121.9 0.1 copy.28
  122.0 0.1 copy.29
  122.1 0.1 copy.30
  122.2 8.2 %all_to_all.41 = f32[4,80,128]{2,1,0:T(8,128)S(1)} all-to-all(f32[4,80,128]{2,1,0:T(8,128)S(1)} %pad_maximum_fusion.1), channel_id=1, replica_groups={{0,8,16,24},{32,40,48,56},{64,72,80,88},{96,104,112,120},{128,136,144,1..., dimensions={0} | all-to-all | bytes 327680 | tf_op jit(solution)/shard_map/all_to_all | solution.py:22
  130.4 0.1 mul.123
  130.5 0.1 fusion.6
  130.7 48.0 %all_to_all.42 = f32[8,80,128]{2,1,0:T(8,128)S(1)} all-to-all(f32[8,80,128]{2,1,0:T(8,128)S(1)} %broadcast_in_dim.77), channel_id=1, replica_groups={{0,32,64,96,128,160,192,224},{8,40,72,104,136,168,200,232},{16,48,80,11..., dimensions={0} | all-to-all | bytes 655360 | tf_op jit(solution)/shard_map/all_to_all | solution.py:22
  178.7 0.1 mul.127
  178.8 0.1 div.15
  178.9 0.1 fusion.5
  179.0 0.1 divide_convert_fusion
  179.1 12.1 %all_to_all.43 = bf16[4,72,128]{2,1,0:T(8,128)(2,1)S(1)} all-to-all(bf16[4,72,128]{2,1,0:T(8,128)(2,1)S(1)} %broadcast_in_dim.78), channel_id=1, replica_groups={{0,8,16,24},{32,40,48,56},{64,72,80,88},{96,104,112,120},{128,136,144,1..., dimensions={0} | all-to-all | bytes 147456 | tf_op jit(solution)/shard_map/all_to_all | solution.py:22
  191.2 0.0 copy-done
  191.2 0.3 convolution_bitcast_fusion.1
  191.5 13.6 %all_to_all.44 = f32[8,3,384]{2,1,0:T(4,128)S(1)} all-to-all(f32[8,3,384]{2,1,0:T(4,128)S(1)} %copy.32), channel_id=1, replica_groups=mesh['parts'=2,'seq'=32,'head'=8] {'head'}, dimensions={0} | all-to-all | bytes 73728 | tf_op jit(solution)/shard_map/all_to_all | solution.py:22
  205.1 0.6 reduce_sum.92
  (33 shorter events, 0.5 us)
Async XLA Ops:
  0.0 191.2 %copy-start = (bf16[1536,384]{1,0:T(8,128)(2,1)S(1)}, bf16[1536,384]{1,0:T(8,128)(2,1)}, u32[]{:S(2)}) copy-start(bf16[1536,384]{1,0:T(8,128)(2,1)} %param.14) | copy-start | bytes 3538948
  1.4 49.4 %all-to-all-start = ((bf16[8,3,384]{2,1,0:T(4,128)(2,1)}), bf16[8,3,384]{2,1,0:T(4,128)(2,1)S(1)}, u32[]{:S(2)}, u32[]{:S(2)}) async-start(bf16[8,3,384]{2,1,0:T(4,128)(2,1)} %broadcast_in_dim.67), calls=%async_computation | async-start | bytes 49152 | tf_op jit(solution)/shard_map/all_to_all | solution.py:22
  46.1 4.8 %copy-start.3 = (bf16[384,128]{1,0:T(8,128)(2,1)S(1)}, bf16[384,128]{1,0:T(8,128)(2,1)}, u32[]{:S(2)}) copy-start(bf16[384,128]{1,0:T(8,128)(2,1)} %param.13) | copy-start | bytes 294916
  46.1 4.8 %copy-start.5 = (f32[384]{0:T(512)S(1)}, f32[384]{0:T(512)}, u32[]{:S(2)}) copy-start(f32[384]{0:T(512)} %param.10) | copy-start | bytes 4612
  46.1 4.9 %copy-start.4 = (bf16[384,128]{1,0:T(8,128)(2,1)S(1)}, bf16[384,128]{1,0:T(8,128)(2,1)}, u32[]{:S(2)}) copy-start(bf16[384,128]{1,0:T(8,128)(2,1)} %param.12) | copy-start | bytes 294916
  60.0 55.8 %copy-start.6 = (s32[24]{0:T(128)S(1)}, s32[24]{0:T(128)}, u32[]{:S(2)}) copy-start(s32[24]{0:T(128)} %param.15) | copy-start | bytes 292
  60.0 60.7 %copy-start.1 = (bf16[24,1,128,128]{3,2,1,0:T(8,128)(2,1)S(1)}, bf16[24,1,128,128]{3,2,1,0:T(8,128)(2,1)}, u32[]{:S(2)}) copy-start(bf16[24,1,128,128]{3,2,1,0:T(8,128)(2,1)} %param.16) | copy-start | bytes 2359300
  60.7 45.2 %all-to-all-start.2 = ((f32[8,88,128]{2,1,0:T(8,128)}), f32[8,88,128]{2,1,0:T(8,128)S(1)}, u32[]{:S(2)}, u32[]{:S(2)}) async-start(f32[8,88,128]{2,1,0:T(8,128)} %broadcast_in_dim.69), calls=%async_computation.2 | async-start | bytes 720896 | tf_op jit(solution)/shard_map/all_to_all | solution.py:22
  106.0 15.5 %copy-start.2 = (bf16[24,1,128,128]{3,2,1,0:T(8,128)(2,1)S(1)}, bf16[24,1,128,128]{3,2,1,0:T(8,128)(2,1)}, u32[]{:S(2)}) copy-start(bf16[24,1,128,128]{3,2,1,0:T(8,128)(2,1)} %param.17) | copy-start | bytes 2359300
  107.0 13.5 %all-to-all-start.3 = ((bf16[4,88,128]{2,1,0:T(8,128)(2,1)}), bf16[4,88,128]{2,1,0:T(8,128)(2,1)S(1)}, u32[]{:S(2)}, u32[]{:S(2)}) async-start(bf16[4,88,128]{2,1,0:T(8,128)(2,1)} %broadcast_in_dim.70), calls=%async_computation.3 | async-start | bytes 180224 | tf_op jit(solution)/shard_map/all_to_all | solution.py:22
